TPU v7x, 128 devices: a whole 4x4x4 slice. The times are simulated.
128 devices in a mesh: space: 128 (over x, y, z, core).
Axes of the slice: x: 4, y: 4, z: 4, core: 2. Of those that a mesh axis runs over, the one named last changes fastest.
Arguments:
- positions: float32 [3, 524288], P(None, 'space'), may hold values from 1 to 512, as said below
- velocity: float32 [3, 524288], P(None, 'space'), may hold values from -5 to 5
- deformation: float32 [9, 524288], P(None, 'space'), may hold values from -0.6 to 1.6
- affine: float32 [9, 524288], P(None, 'space'), may hold values from -3 to 3
- particle_mass: float32 [524288], P('space'), may hold values from 0.05 to 0.3
- volume: float32 [524288], P('space'), may hold values from 0.06 to 0.25
- bin_block: int32 [1024], P('space'), may hold values from 0 to 255
- live_count: int32 [128], P('space'), may hold values from 2 to 4, as said below
Outputs:
- displacement: float32 [3, 524288], P(None, 'space')
- new_velocity: float32 [3, 524288], P(None, 'space')
- new_deformation: float32 [9, 524288], P(None, 'space')
- new_affine: float32 [9, 524288], P(None, 'space')
Inputs may be any that keep to these rules, and one draw needn't show every extreme that they name: `positions`: each particle lies inside its bin's block: 4 d + 1 to 4 d + 4 along the first dimension for the bins of device d, 4 (bin_block // 16) + 1 to 4 (bin_block // 16) + 4 along the second, 4 (bin_block % 16) + 1 to 4 (bin_block % 16) + 4 along the third. The live bins of device d are its first live_count[d] slots; devices 2 k and 2 k + 1 hold at most 6 live bins together, and some such pair holds exactly 6 in every draw.
All inputs are finite; a program needn't handle non-finite values.
Results may differ from a plain program's by a relative error of at most 0.0003.
Values sent between devices are 32-bit elements; how exact they have to be, the bound alone decides.
A program may use at most 128 MiB of HBM per device.

v0:
```python
import functools

import jax
import jax.numpy as jnp
from jax import lax
from jax.sharding import Mesh
from jax.sharding import PartitionSpec as P

BZ = 16
STEPS = 3
NGY = 66
NGZ = 66
SPACE = ("space_0", "space_1", "space_2", "space_3")


mu_shear = 4.0
lame_first = 6.0
courant = 0.15
sound_speed = 3.7416573867739413
mass_floor = 0.05
gravity_x = 3.0
gravity_z = -9.0
highest = lax.Precision.HIGHEST


def swapped(value, axis, bit):
    mask = 2**bit
    pairs = [(source, source ^ mask) for source in range(lax.axis_size(axis))]
    return lax.ppermute(value, axis, pairs)


def by_axis(value, axes):
    return functools.reduce(lax.pmax, axes, value)


def passed_along(value, axis, by):
    length = lax.axis_size(axis)
    pairs = [(i, i + by) for i in range(length) if 0 <= i + by < length]
    return lax.ppermute(value, axis, pairs)


def spline(distance):
    magnitude = jnp.abs(distance)
    inner_part = 0.75 - magnitude * magnitude
    outer_part = 0.5 * (1.5 - magnitude) * (1.5 - magnitude)
    return jnp.where(
        magnitude < 0.5, inner_part, jnp.where(magnitude < 1.5, outer_part, 0.0 * magnitude)
    )


def node_coords():
    numbers = jnp.arange(216, dtype=jnp.int32)
    return jnp.stack([numbers // 36, numbers // 6 % 6, numbers % 6]).astype(jnp.float32)


def spline_weights(local_coords):
    offsets = jnp.arange(6, dtype=jnp.int32).astype(jnp.float32)
    per_axis = [
        spline(offsets[None, :, None] - local_coords[number][:, None, :]) for number in range(3)
    ]
    weight_table = (
        per_axis[0][:, :, None, None, :]
        * per_axis[1][:, None, :, None, :]
        * per_axis[2][:, None, None, :, :]
    )
    return weight_table.reshape(local_coords.shape[1], 216, local_coords.shape[2])


def block_anchor(home_devices, blocks):
    return jnp.stack([4 * home_devices, 4 * (blocks // BZ), 4 * (blocks % BZ)]).astype(jnp.float32)


def selectors(starts, node_total):
    columns = jnp.arange(node_total, dtype=jnp.int32)
    offsets = jnp.arange(6, dtype=jnp.int32)
    return (columns[None, None, :] == 4 * starts[:, None, None] + offsets[None, :, None]).astype(
        jnp.float32
    )


def plane_selector(select_y, select_z):
    joined = select_y[:, :, None, :, None] * select_z[:, None, :, None, :]
    return joined.reshape(select_y.shape[0], 36, select_y.shape[2] * select_z.shape[2])


def kirchhoff(deform):
    entries = [deform[number] for number in range(9)]
    determinant = (
        entries[0] * (entries[4] * entries[8] - entries[5] * entries[7])
        - entries[1] * (entries[3] * entries[8] - entries[5] * entries[6])
        + entries[2] * (entries[3] * entries[7] - entries[4] * entries[6])
    )
    pressure_term = lame_first * (determinant - 1.0) * determinant
    stress = []
    for outer_index in range(3):
        for inner_index in range(3):
            product = (
                entries[3 * outer_index] * entries[3 * inner_index]
                + entries[3 * outer_index + 1] * entries[3 * inner_index + 1]
                + entries[3 * outer_index + 2] * entries[3 * inner_index + 2]
            )
            if outer_index == inner_index:
                stress.append(mu_shear * (product - 1.0) + pressure_term)
            else:
                stress.append(mu_shear * product)
    return stress


def particle_to_grid(working, local_coords, weight_table, time_step):
    stress = kirchhoff(working[6:15])
    masses = working[24]
    volumes = working[25]
    affine_term = [
        masses * working[15 + number] - 4.0 * time_step * volumes * stress[number]
        for number in range(9)
    ]
    momentum = []
    for outer_index in range(3):
        shifted = masses * working[3 + outer_index]
        for inner_index in range(3):
            shifted = (
                shifted - affine_term[3 * outer_index + inner_index] * local_coords[inner_index]
            )
        momentum.append(shifted)
    quantities = jnp.stack([masses] + momentum + affine_term)
    summed = jnp.einsum("cbp,bnp->bcn", quantities, weight_table, precision=highest)
    nodes = node_coords()
    moments = []
    for outer_index in range(3):
        total_moment = summed[:, 1 + outer_index]
        for inner_index in range(3):
            total_moment = (
                total_moment
                + summed[:, 4 + 3 * outer_index + inner_index] * nodes[inner_index][None, :]
            )
        moments.append(total_moment)
    return jnp.stack([summed[:, 0]] + moments, axis=1)


def scatter_tiles(node_tiles, select_plane, grid_y, grid_z):
    shaped = node_tiles.reshape(node_tiles.shape[0], 24, 36)
    spread = jnp.einsum("bqn,bnm->qm", shaped, select_plane, precision=highest)
    return spread.reshape(4, 6, grid_y, grid_z)


def tile_velocities(slab_velocity, select_plane):
    flat = slab_velocity.reshape(18, select_plane.shape[2])
    gathered = jnp.einsum("qm,bnm->bqn", flat, select_plane, precision=highest)
    return gathered.reshape(gathered.shape[0], 3, 216)


def grid_velocity(owned_planes, device, time_step, plane_total):
    node_mass = jnp.maximum(owned_planes[0], mass_floor)
    planes = 4 * device + jnp.arange(4, dtype=jnp.int32)
    column_y = jnp.arange(owned_planes.shape[2], dtype=jnp.int32)
    column_z = jnp.arange(owned_planes.shape[3], dtype=jnp.int32)
    along_x = owned_planes[1] / node_mass + time_step * gravity_x
    along_y = owned_planes[2] / node_mass
    along_z = owned_planes[3] / node_mass + time_step * gravity_z
    along_x = jnp.where((planes < 2)[:, None, None], jnp.maximum(along_x, 0.0), along_x)
    along_x = jnp.where(
        (planes >= plane_total - 2)[:, None, None], jnp.minimum(along_x, 0.0), along_x
    )
    along_y = jnp.where((column_y < 2)[None, :, None], jnp.maximum(along_y, 0.0), along_y)
    along_y = jnp.where(
        (column_y >= owned_planes.shape[2] - 2)[None, :, None], jnp.minimum(along_y, 0.0), along_y
    )
    along_z = jnp.where((column_z < 2)[None, None, :], jnp.maximum(along_z, 0.0), along_z)
    along_z = jnp.where(
        (column_z >= owned_planes.shape[3] - 2)[None, None, :], jnp.minimum(along_z, 0.0), along_z
    )
    return jnp.stack([along_x, along_y, along_z])


def grid_to_particle(working, local_coords, weight_table, velocity_tiles, time_step):
    nodes = node_coords()
    node_terms = [velocity_tiles[:, number] for number in range(3)]
    for outer_index in range(3):
        for inner_index in range(3):
            node_terms.append(velocity_tiles[:, outer_index] * nodes[inner_index][None, :])
    stacked = jnp.stack(node_terms, axis=1)
    interpolated = jnp.einsum("bcn,bnp->cbp", stacked, weight_table, precision=highest)
    new_motion = interpolated[0:3]
    affine_new = []
    for outer_index in range(3):
        for inner_index in range(3):
            affine_new.append(
                4.0
                * (
                    interpolated[3 + 3 * outer_index + inner_index]
                    - new_motion[outer_index] * local_coords[inner_index]
                )
            )
    deform = working[6:15]
    deform_new = []
    for outer_index in range(3):
        for inner_index in range(3):
            updated = deform[3 * outer_index + inner_index]
            for middle_index in range(3):
                updated = (
                    updated
                    + time_step
                    * affine_new[3 * outer_index + middle_index]
                    * deform[3 * middle_index + inner_index]
                )
            deform_new.append(updated)
    moved = working[0:3] + time_step * new_motion
    travelled = working[26:29] + time_step * new_motion
    return jnp.concatenate(
        [moved, new_motion, jnp.stack(deform_new), jnp.stack(affine_new), working[24:26], travelled]
    )


def parity_part(array, axis, parity):
    shape = array.shape
    split = array.reshape(shape[:axis] + (shape[axis] // 2, 2) + shape[axis + 1 :])
    first = lax.index_in_dim(split, 0, axis + 1, keepdims=False)
    second = lax.index_in_dim(split, 1, axis + 1, keepdims=False)
    return jnp.where(parity == 0, first, second)


def by_parity(mine, other, axis, parity):
    even_part = jnp.where(parity == 0, mine, other)
    odd_part = jnp.where(parity == 0, other, mine)
    stacked = jnp.stack([even_part, odd_part], axis=axis + 1)
    shape = mine.shape
    return stacked.reshape(shape[:axis] + (2 * shape[axis],) + shape[axis + 1 :])


def local(positions, velocity, deformation, affine, particle_mass, volume, bin_block, live_count):
    slot_total = bin_block.shape[0]
    per_bin = positions.shape[1] // slot_total
    half_slots = slot_total // 2
    device = lax.axis_index(SPACE)
    partner = jnp.bitwise_xor(device, 1)
    parity = jnp.bitwise_and(device, 1)
    plane_total = 4 * lax.axis_size(SPACE)
    slot_ids = jnp.arange(slot_total, dtype=jnp.int32)
    live_slots = (slot_ids < live_count[0]).astype(jnp.float32)
    kept_total = (live_count[0] + 1 - parity) // 2
    own_first = jnp.arange(half_slots, dtype=jnp.int32) < kept_total
    masked_mass = particle_mass.reshape(1, slot_total, per_bin) * live_slots[None, :, None]
    masked_volume = volume.reshape(1, slot_total, per_bin) * live_slots[None, :, None]
    grouped = jnp.concatenate([positions, velocity, deformation, affine]).reshape(
        24, slot_total, per_bin
    )
    travelled = jnp.zeros((3, slot_total, per_bin), jnp.float32)
    packed = jnp.concatenate([grouped, masked_mass, masked_volume, travelled])
    home_plane = plane_selector(selectors(bin_block // BZ, NGY), selectors(bin_block % BZ, NGZ))
    partner_homes = jnp.where(own_first, device, partner)
    sending = parity_part(packed, 1, 1 - parity)
    sending_blocks = parity_part(bin_block, 0, 1 - parity).astype(jnp.float32)
    received, received_blocks = swapped((sending, sending_blocks), SPACE, 0)
    working = jnp.where(own_first[None, :, None], parity_part(packed, 1, parity), received[:, ::-1])
    blocks = jnp.where(
        own_first, parity_part(bin_block, 0, parity), received_blocks[::-1].astype(jnp.int32)
    )
    working, blocks = (working, blocks)
    for iteration in range(STEPS):
        speed_squared = jnp.where(
            working[24] > 0.0, jnp.sum(working[3:6] * working[3:6], axis=0), 0.0
        )
        fastest = by_axis(jnp.max(speed_squared), SPACE)
        time_step = courant / (jnp.sqrt(fastest) + sound_speed)
        anchor = block_anchor(partner_homes, blocks)
        local_coords = working[0:3] - anchor[:, :, None]
        weight_table = spline_weights(local_coords)
        node_tiles = particle_to_grid(working, local_coords, weight_table, time_step)
        returned = swapped(node_tiles, SPACE, 0)
        node_tiles = by_parity(node_tiles, returned[::-1], 0, parity) * live_slots[:, None, None]
        partial_slab = scatter_tiles(node_tiles, home_plane, NGY, NGZ)
        incoming = passed_along(partial_slab[:, 4:6], SPACE, 1)
        owned_planes = jnp.concatenate(
            [partial_slab[:, 0:2] + incoming, partial_slab[:, 2:4]], axis=1
        )
        grid_motion = grid_velocity(owned_planes, device, time_step, plane_total)
        ghost_planes = passed_along(grid_motion[:, 0:2], SPACE, -1)
        slab_velocity = jnp.concatenate([grid_motion, ghost_planes], axis=1)
        velocity_tiles = tile_velocities(slab_velocity, home_plane)
        partner_tiles = swapped(parity_part(velocity_tiles, 0, 1 - parity), SPACE, 0)
        velocity_tiles = jnp.where(
            own_first[:, None, None], parity_part(velocity_tiles, 0, parity), partner_tiles[::-1]
        )
        working = grid_to_particle(working, local_coords, weight_table, velocity_tiles, time_step)
    kept_rows = jnp.concatenate([working[0:24], working[26:29]])
    received = swapped(kept_rows, SPACE, 0)
    gathered = by_parity(kept_rows, received[:, ::-1], 1, parity)
    finished = jnp.concatenate([gathered[24:27], gathered[3:24]])
    finished = finished * live_slots[None, :, None]
    flattened = finished.reshape(24, slot_total * per_bin)
    return (flattened[0:3], flattened[3:6], flattened[6:15], flattened[15:24])


def solution(mesh):
    split = Mesh(mesh.devices.reshape(4, 4, 4, 2), ("space_0", "space_1", "space_2", "space_3"))
    placed = (
        P(None, SPACE),
        P(None, SPACE),
        P(None, SPACE),
        P(None, SPACE),
        P(SPACE),
        P(SPACE),
        P(SPACE),
        P(SPACE),
    )
    return jax.shard_map(
        local,
        mesh=split,
        in_specs=placed,
        out_specs=(P(None, SPACE), P(None, SPACE), P(None, SPACE), P(None, SPACE)),
        check_vma=False,
    )
```

profile of v0, /device:TPU:3, one launch (start us, length us, event | category | flops | bytes accessed | tf_op | source)
XLA Modules:
  0.0 318.3 jit_solution(14827397247795740752)
XLA Ops:
  6.3 5.4 %broadcast_multiply_fusion = f32[8,6,6,66,66]{4,3,0,2,1:T(8,128)} fusion(f32[8,6,66]{2,0,1:T(8,128)S(1)} %fusion.139, f32[8,6,66]{2,0,1:T(8,128)S(1)} %fusion.138), kind=kLoop, calls=%fused_computation.15 | loop fusion | flops 1254528 | bytes 5043456 | tf_op jit(solution)/shard_map/mul | solution.py:82
  13.1 7.2 %pmax.84 = f32[]{:T(128)} all-reduce(f32[]{:T(128)} %get-tuple-element.82), channel_id=1, replica_groups=mesh['space_0'=4,'space_1'=4,'space_2'=4,'space_3'=2] {'space_0'}, use_global_device_ids=true, to_apply=%region_2.3 | all-reduce | flops 1 | bytes 8 | tf_op jit(solution)/shard_map/pmax | solution.py:33
  20.3 9.4 %pmax.85 = f32[]{:T(128)} all-reduce(f32[]{:T(128)} %pmax.84), channel_id=1, replica_groups=mesh['space_0'=4,'space_1'=4,'space_2'=4,'space_3'=2] {'space_1'}, use_global_device_ids=true, to_apply=%region_3.4 | all-reduce | flops 1 | bytes 8 | tf_op jit(solution)/shard_map/pmax | solution.py:33
  29.7 10.4 %pmax.86 = f32[]{:T(128)} all-reduce(f32[]{:T(128)} %pmax.85), channel_id=1, replica_groups=mesh['space_0'=4,'space_1'=4,'space_2'=4,'space_3'=2] {'space_2'}, use_global_device_ids=true, to_apply=%region_4.5 | all-reduce | flops 1 | bytes 8 | tf_op jit(solution)/shard_map/pmax | solution.py:33
  40.7 9.3 %pmax.87 = f32[]{:T(128)} all-reduce(f32[]{:T(128)} %pmax.86), channel_id=1, replica_groups=mesh['space_0'=4,'space_1'=4,'space_2'=4,'space_3'=2] {'space_3'}, use_global_device_ids=true, to_apply=%region_5.6 | all-reduce | flops 1 | bytes 8 | tf_op jit(solution)/shard_map/pmax | solution.py:33
  54.3 9.8 %mul.4946 = f32[8,36,4356]{2,0,1:T(8,128)} reshape(f32[8,6,6,66,66]{4,3,0,2,1:T(8,128)} %broadcast_multiply_fusion) | data formatting | bytes 10036224 | tf_op jit(solution)/shard_map/mul | solution.py:82
  64.1 9.9 %dot_general.56 = f32[66,66,8,36]{1,0,2,3:T(8,128)} reshape(f32[4356,8,36]{0,1,2:T(8,128)} %bitcast.181) | data formatting | bytes 10036224 | tf_op jit(solution)/shard_map/bqn,bnm->qm/dot_general | solution.py:142
  74.2 14.8 %fusion.27 = f32[4,6,66,66]{3,1,2,0:T(8,128)S(1)} fusion(f32[66,66,8,36]{1,0,2,3:T(8,128)} %dot_general.56, f32[4,6,8,36,1]{3,2,1,0,4:T(8,128)S(1)} %bitcast.208), kind=kOutput, calls=%fused_computation.28 | convolution fusion | flops 361304064 | bytes 5463936 | tf_op jit(solution)/shard_map/bqn,bnm->qm/dot_general | solution.py:142
  91.9 3.6 %collective-permute-done.3 = f32[4,2,66,66]{3,1,2,0:T(2,128)} collective-permute-done((f32[4,2,66,66]{3,1,2,0:T(2,128)}, f32[4,2,66,66]{3,1,2,0:T(2,128)}, u32[]{:S(2)}, u32[]{:S(2)}) %collective-permute-start.3) | collective-permute-done | bytes 139424 | tf_op jit(solution)/shard_map/ppermute | solution.py:39
  97.4 9.0 %collective-permute-start.4 = (f32[3,2,66,66]{3,1,2,0:T(2,128)S(1)}, f32[3,2,66,66]{3,1,2,0:T(2,128)S(1)}, u32[]{:S(2)}, u32[]{:S(2)}) collective-permute-start(f32[3,2,66,66]{3,1,2,0:T(2,128)S(1)} %pad_maximum_fusion.9), channel_id=1, source_target_pairs={{1,0},{2,1},{3,2},{4,3},{5,4},{6,5},{7,6},{8,7},{9,8},{10,9},{11,1... | collective-permute-start | bytes 313640 | tf_op jit(solution)/shard_map/ppermute | solution.py:39
  107.9 12.2 %fusion.36 = f32[8,18,36]{2,1,0:T(8,128)S(1)} fusion(f32[18,4356,1]{1,0,2:T(8,128)S(1)} %reshape.867, f32[8,36,4356]{2,0,1:T(8,128)} %mul.4946), kind=kOutput, calls=%fused_computation.31 | convolution fusion | flops 270978048 | bytes 5352480 | tf_op jit(solution)/shard_map/qm,bnm->bqn/dot_general | solution.py:148
  120.2 2.3 collective-permute-start.5
  125.7 6.9 %pmax.88 = f32[]{:T(128)} all-reduce(f32[]{:T(128)} %select_reduce_fusion.1), channel_id=1, replica_groups=mesh['space_0'=4,'space_1'=4,'space_2'=4,'space_3'=2] {'space_0'}, use_global_device_ids=true, to_apply=%region_8.9 | all-reduce | flops 1 | bytes 8 | tf_op jit(solution)/shard_map/pmax | solution.py:33
  132.6 6.6 %pmax.89 = f32[]{:T(128)} all-reduce(f32[]{:T(128)} %pmax.88), channel_id=1, replica_groups=mesh['space_0'=4,'space_1'=4,'space_2'=4,'space_3'=2] {'space_1'}, use_global_device_ids=true, to_apply=%region_9.10 | all-reduce | flops 1 | bytes 8 | tf_op jit(solution)/shard_map/pmax | solution.py:33
  139.2 12.9 %pmax.90 = f32[]{:T(128)} all-reduce(f32[]{:T(128)} %pmax.89), channel_id=1, replica_groups=mesh['space_0'=4,'space_1'=4,'space_2'=4,'space_3'=2] {'space_2'}, use_global_device_ids=true, to_apply=%region_10.11 | all-reduce | flops 1 | bytes 8 | tf_op jit(solution)/shard_map/pmax | solution.py:33
  152.2 9.4 %pmax.91 = f32[]{:T(128)} all-reduce(f32[]{:T(128)} %pmax.90), channel_id=1, replica_groups=mesh['space_0'=4,'space_1'=4,'space_2'=4,'space_3'=2] {'space_3'}, use_global_device_ids=true, to_apply=%region_11.12 | all-reduce | flops 1 | bytes 8 | tf_op jit(solution)/shard_map/pmax | solution.py:33
  163.9 1.9 fusion.19
  167.6 14.8 %fusion.30 = f32[4,6,66,66]{3,1,2,0:T(8,128)S(1)} fusion(f32[66,66,8,36]{1,0,2,3:T(8,128)} %dot_general.56, f32[4,6,8,36,1]{3,2,1,0,4:T(8,128)S(1)} %bitcast.209), kind=kOutput, calls=%fused_computation.29 | convolution fusion | flops 361304064 | bytes 5463936 | tf_op jit(solution)/shard_map/bqn,bnm->qm/dot_general | solution.py:142
  185.2 3.7 %collective-permute-done.7 = f32[4,2,66,66]{3,1,2,0:T(2,128)} collective-permute-done((f32[4,2,66,66]{3,1,2,0:T(2,128)}, f32[4,2,66,66]{3,1,2,0:T(2,128)}, u32[]{:S(2)}, u32[]{:S(2)}) %collective-permute-start.7) | collective-permute-done | bytes 139424 | tf_op jit(solution)/shard_map/ppermute | solution.py:39
  190.8 9.1 %collective-permute-start.8 = (f32[3,2,66,66]{3,1,2,0:T(2,128)S(1)}, f32[3,2,66,66]{3,1,2,0:T(2,128)S(1)}, u32[]{:S(2)}, u32[]{:S(2)}) collective-permute-start(f32[3,2,66,66]{3,1,2,0:T(2,128)S(1)} %pad_maximum_fusion.7), channel_id=1, source_target_pairs={{1,0},{2,1},{3,2},{4,3},{5,4},{6,5},{7,6},{8,7},{9,8},{10,9},{11,1... | collective-permute-start | bytes 313640 | tf_op jit(solution)/shard_map/ppermute | solution.py:39
  201.4 12.1 %fusion.39 = f32[8,18,36]{2,1,0:T(8,128)S(1)} fusion(f32[18,4356,1]{1,0,2:T(8,128)S(1)} %reshape.871, f32[8,36,4356]{2,0,1:T(8,128)} %mul.4946), kind=kOutput, calls=%fused_computation.32 | convolution fusion | flops 270978048 | bytes 5352480 | tf_op jit(solution)/shard_map/qm,bnm->bqn/dot_general | solution.py:148
  213.8 2.3 collective-permute-start.9
  219.4 5.7 %pmax.92 = f32[]{:T(128)} all-reduce(f32[]{:T(128)} %select_reduce_fusion), channel_id=1, replica_groups=mesh['space_0'=4,'space_1'=4,'space_2'=4,'space_3'=2] {'space_0'}, use_global_device_ids=true, to_apply=%region_14.15 | all-reduce | flops 1 | bytes 8 | tf_op jit(solution)/shard_map/pmax | solution.py:33
  225.1 6.6 %pmax.93 = f32[]{:T(128)} all-reduce(f32[]{:T(128)} %pmax.92), channel_id=1, replica_groups=mesh['space_0'=4,'space_1'=4,'space_2'=4,'space_3'=2] {'space_1'}, use_global_device_ids=true, to_apply=%region_15.16 | all-reduce | flops 1 | bytes 8 | tf_op jit(solution)/shard_map/pmax | solution.py:33
  231.7 14.1 %pmax.94 = f32[]{:T(128)} all-reduce(f32[]{:T(128)} %pmax.93), channel_id=1, replica_groups=mesh['space_0'=4,'space_1'=4,'space_2'=4,'space_3'=2] {'space_2'}, use_global_device_ids=true, to_apply=%region_16.17 | all-reduce | flops 1 | bytes 8 | tf_op jit(solution)/shard_map/pmax | solution.py:33
  245.9 9.2 %pmax.95 = f32[]{:T(128)} all-reduce(f32[]{:T(128)} %pmax.94), channel_id=1, replica_groups=mesh['space_0'=4,'space_1'=4,'space_2'=4,'space_3'=2] {'space_3'}, use_global_device_ids=true, to_apply=%region_17.18 | all-reduce | flops 1 | bytes 8 | tf_op jit(solution)/shard_map/pmax | solution.py:33
  256.9 1.9 fusion.15
  260.5 14.8 %fusion.33 = f32[4,6,66,66]{3,1,2,0:T(8,128)S(1)} fusion(f32[66,66,8,36]{1,0,2,3:T(8,128)} %dot_general.56, f32[4,6,8,36,1]{3,2,1,0,4:T(8,128)S(1)} %bitcast.207), kind=kOutput, calls=%fused_computation.30 | convolution fusion | flops 361304064 | bytes 5463936 | tf_op jit(solution)/shard_map/bqn,bnm->qm/dot_general | solution.py:142
  278.1 3.7 %collective-permute-done.11 = f32[4,2,66,66]{3,1,2,0:T(2,128)} collective-permute-done((f32[4,2,66,66]{3,1,2,0:T(2,128)}, f32[4,2,66,66]{3,1,2,0:T(2,128)}, u32[]{:S(2)}, u32[]{:S(2)}) %collective-permute-start.11) | collective-permute-done | bytes 139424 | tf_op jit(solution)/shard_map/ppermute | solution.py:39
  283.7 9.2 %collective-permute-start.12 = (f32[3,2,66,66]{3,1,2,0:T(2,128)S(1)}, f32[3,2,66,66]{3,1,2,0:T(2,128)S(1)}, u32[]{:S(2)}, u32[]{:S(2)}) collective-permute-start(f32[3,2,66,66]{3,1,2,0:T(2,128)S(1)} %pad_maximum_fusion.5), channel_id=1, source_target_pairs={{1,0},{2,1},{3,2},{4,3},{5,4},{6,5},{7,6},{8,7},{9,8},{10,9},{11,1... | collective-permute-start | bytes 313640 | tf_op jit(solution)/shard_map/ppermute | solution.py:39
  294.3 12.1 %fusion.42 = f32[8,18,36]{2,1,0:T(8,128)S(1)} fusion(f32[18,4356,1]{1,0,2:T(8,128)S(1)} %reshape.875, f32[8,36,4356]{2,0,1:T(8,128)} %mul.4946), kind=kOutput, calls=%fused_computation.33 | convolution fusion | flops 270978048 | bytes 5352480 | tf_op jit(solution)/shard_map/qm,bnm->bqn/dot_general | solution.py:148
  306.6 2.3 collective-permute-start.13
  (310 shorter events, 50.3 us)
Async XLA Ops:
  4.7 7.2 %collective-permute-start = (f32[29,4,512]{2,1,0:T(4,128)S(1)}, f32[29,4,512]{2,1,0:T(4,128)S(1)}, u32[]{:S(2)}, u32[]{:S(2)}) collective-permute-start(f32[29,4,512]{2,1,0:T(4,128)S(1)} %select_bitcast_fusion), channel_id=1, source_target_pairs={{0,1},{1,0},{2,3},{3,2},{4,5},{5,4},{6,7},{7,6},{8,9},{9,8},{10,11... | collective-permute-start | bytes 712712 | tf_op jit(solution)/shard_map/ppermute | solution.py:29
  5.8 6.0 %collective-permute-start.1 = (f32[4]{0:T(128)S(1)}, f32[4]{0:T(128)S(1)}, u32[]{:S(2)}, u32[]{:S(2)}) collective-permute-start(f32[4]{0:T(128)S(1)} %convert_reduce_fusion), channel_id=1, source_target_pairs={{0,1},{1,0},{2,3},{3,2},{4,5},{5,4},{6,7},{7,6},{8,9},{9,8},{10,11... | collective-permute-start | bytes 56 | tf_op jit(solution)/shard_map/ppermute | solution.py:29
  6.0 117.3 %copy-start.30 = (pred[4]{0:T(512)(128)(4,1)}, pred[4]{0:T(512)(128)(4,1)S(1)}, u32[]{:S(2)}) copy-start(pred[4]{0:T(512)(128)(4,1)S(1)} %iota_compare_fusion.4) | copy-start | bytes 16
  11.7 205.3 %copy-start.13 = (f32[1,216]{1,0:T(1,128)}, f32[1,216]{1,0:T(1,128)S(1)}, u32[]{:S(2)}) copy-start(f32[1,216]{1,0:T(1,128)S(1)} %get-tuple-element.182) | copy-start | bytes 2596
  11.7 205.3 %copy-start.15 = (f32[1,216]{1,0:T(1,128)}, f32[1,216]{1,0:T(1,128)S(1)}, u32[]{:S(2)}) copy-start(f32[1,216]{1,0:T(1,128)S(1)} %get-tuple-element.183) | copy-start | bytes 2596
  11.9 113.1 %copy-start.20 = (f32[3,4]{1,0:T(4,128)}, f32[3,4]{1,0:T(4,128)S(1)}, u32[]{:S(2)}) copy-start(f32[3,4]{1,0:T(4,128)S(1)} %add_convert_fusion) | copy-start | bytes 148
  13.1 112.0 %copy-start.22 = (pred[1,4,512]{2,1,0:T(4,128)(4,1)}, pred[1,4,512]{2,1,0:T(4,128)(4,1)S(1)}, u32[]{:S(2)}) copy-start(pred[1,4,512]{2,1,0:T(4,128)(4,1)S(1)} %get-tuple-element.83) | copy-start | bytes 6148
  53.7 20.3 %collective-permute-start.2 = (f32[4,4,216]{2,1,0:T(4,128)S(1)}, f32[4,4,216]{2,1,0:T(4,128)S(1)}, u32[]{:S(2)}, u32[]{:S(2)}) collective-permute-start(f32[4,4,216]{2,1,0:T(4,128)S(1)} %pad_maximum_fusion.18), channel_id=1, source_target_pairs={{0,1},{1,0},{2,3},{3,2},{4,5},{5,4},{6,7},{7,6},{8,9},{9,8},{10,11... | collective-permute-start | bytes 41480 | tf_op jit(solution)/shard_map/ppermute | solution.py:29
  89.9 5.6 %collective-permute-start.3 = (f32[4,2,66,66]{3,1,2,0:T(2,128)}, f32[4,2,66,66]{3,1,2,0:T(2,128)}, u32[]{:S(2)}, u32[]{:S(2)}) collective-permute-start(f32[4,2,66,66]{3,1,2,0:T(2,128)} %slice.974), channel_id=1, source_target_pairs={{0,1},{1,2},{2,3},{3,4},{4,5},{5,6},{6,7},{7,8},{8,9},{9,10},{10,1... | collective-permute-start | bytes 418184 | tf_op jit(solution)/shard_map/ppermute | solution.py:39
  97.4 9.8 %collective-permute-start.4 = (f32[3,2,66,66]{3,1,2,0:T(2,128)S(1)}, f32[3,2,66,66]{3,1,2,0:T(2,128)S(1)}, u32[]{:S(2)}, u32[]{:S(2)}) collective-permute-start(f32[3,2,66,66]{3,1,2,0:T(2,128)S(1)} %pad_maximum_fusion.9), channel_id=1, source_target_pairs={{1,0},{2,1},{3,2},{4,3},{5,4},{6,5},{7,6},{8,7},{9,8},{10,9},{11,1... | collective-permute-start | bytes 313640 | tf_op jit(solution)/shard_map/ppermute | solution.py:39
  120.0 42.3 %copy-start = (f32[13,4,512]{2,1,0:T(4,128)S(1)}, f32[13,4,512]{2,1,0:T(4,128)}, u32[]{:S(2)}) copy-start(f32[13,4,512]{2,1,0:T(4,128)} %copy.189) | copy-start | bytes 319492
  120.2 3.1 collective-permute-start.5
  123.4 39.9 %copy-start.38 = (f32[6]{0:T(128)S(1)}, f32[6]{0:T(128)}, u32[]{:S(2)}) copy-start(f32[6]{0:T(128)} %copy-done.37) | copy-start | bytes 76
  166.0 1.3 collective-permute-start.6
  183.3 5.6 %collective-permute-start.7 = (f32[4,2,66,66]{3,1,2,0:T(2,128)}, f32[4,2,66,66]{3,1,2,0:T(2,128)}, u32[]{:S(2)}, u32[]{:S(2)}) collective-permute-start(f32[4,2,66,66]{3,1,2,0:T(2,128)} %slice.1017), channel_id=1, source_target_pairs={{0,1},{1,2},{2,3},{3,4},{4,5},{5,6},{6,7},{7,8},{8,9},{9,10},{10,1... | collective-permute-start | bytes 418184 | tf_op jit(solution)/shard_map/ppermute | solution.py:39
  190.8 10.0 %collective-permute-start.8 = (f32[3,2,66,66]{3,1,2,0:T(2,128)S(1)}, f32[3,2,66,66]{3,1,2,0:T(2,128)S(1)}, u32[]{:S(2)}, u32[]{:S(2)}) collective-permute-start(f32[3,2,66,66]{3,1,2,0:T(2,128)S(1)} %pad_maximum_fusion.7), channel_id=1, source_target_pairs={{1,0},{2,1},{3,2},{4,3},{5,4},{6,5},{7,6},{8,7},{9,8},{10,9},{11,1... | collective-permute-start | bytes 313640 | tf_op jit(solution)/shard_map/ppermute | solution.py:39
  213.6 42.1 %copy-start.2 = (f32[1,4,512]{2,1,0:T(4,128)S(1)}, f32[1,4,512]{2,1,0:T(4,128)}, u32[]{:S(2)}) copy-start(f32[1,4,512]{2,1,0:T(4,128)} %copy-done.1) | copy-start | bytes 24580
  213.6 42.1 %copy-start.4 = (f32[1,4,512]{2,1,0:T(4,128)S(1)}, f32[1,4,512]{2,1,0:T(4,128)}, u32[]{:S(2)}) copy-start(f32[1,4,512]{2,1,0:T(4,128)} %copy-done.3) | copy-start | bytes 24580
  213.6 42.1 %copy-start.6 = (f32[1,4,512]{2,1,0:T(4,128)S(1)}, f32[1,4,512]{2,1,0:T(4,128)}, u32[]{:S(2)}) copy-start(f32[1,4,512]{2,1,0:T(4,128)} %copy-done.5) | copy-start | bytes 24580
  213.6 42.1 %copy-start.8 = (f32[1,4,512]{2,1,0:T(4,128)S(1)}, f32[1,4,512]{2,1,0:T(4,128)}, u32[]{:S(2)}) copy-start(f32[1,4,512]{2,1,0:T(4,128)} %copy-done.7) | copy-start | bytes 24580
  213.7 42.1 %copy-start.10 = (f32[1,4,512]{2,1,0:T(4,128)S(1)}, f32[1,4,512]{2,1,0:T(4,128)}, u32[]{:S(2)}) copy-start(f32[1,4,512]{2,1,0:T(4,128)} %copy-done.9) | copy-start | bytes 24580
  213.7 42.1 %copy-start.12 = (f32[1,4,512]{2,1,0:T(4,128)S(1)}, f32[1,4,512]{2,1,0:T(4,128)}, u32[]{:S(2)}) copy-start(f32[1,4,512]{2,1,0:T(4,128)} %copy-done.11) | copy-start | bytes 24580
  213.7 42.1 %copy-start.17 = (f32[1,4,512]{2,1,0:T(4,128)S(1)}, f32[1,4,512]{2,1,0:T(4,128)}, u32[]{:S(2)}) copy-start(f32[1,4,512]{2,1,0:T(4,128)} %get-tuple-element.53) | copy-start | bytes 24580
  213.7 42.1 %copy-start.18 = (f32[1,4,512]{2,1,0:T(4,128)S(1)}, f32[1,4,512]{2,1,0:T(4,128)}, u32[]{:S(2)}) copy-start(f32[1,4,512]{2,1,0:T(4,128)} %get-tuple-element.56) | copy-start | bytes 24580
  213.7 42.1 %copy-start.19 = (f32[1,4,512]{2,1,0:T(4,128)S(1)}, f32[1,4,512]{2,1,0:T(4,128)}, u32[]{:S(2)}) copy-start(f32[1,4,512]{2,1,0:T(4,128)} %get-tuple-element.67) | copy-start | bytes 24580
  213.8 3.1 collective-permute-start.9
  217.0 39.1 %copy-start.39 = (f32[6]{0:T(128)S(1)}, f32[6]{0:T(128)}, u32[]{:S(2)}) copy-start(f32[6]{0:T(128)} %copy-done.37) | copy-start | bytes 76
  258.9 1.3 collective-permute-start.10
  276.2 5.6 %collective-permute-start.11 = (f32[4,2,66,66]{3,1,2,0:T(2,128)}, f32[4,2,66,66]{3,1,2,0:T(2,128)}, u32[]{:S(2)}, u32[]{:S(2)}) collective-permute-start(f32[4,2,66,66]{3,1,2,0:T(2,128)} %slice.1060), channel_id=1, source_target_pairs={{0,1},{1,2},{2,3},{3,4},{4,5},{5,6},{6,7},{7,8},{8,9},{9,10},{10,1... | collective-permute-start | bytes 418184 | tf_op jit(solution)/shard_map/ppermute | solution.py:39
  283.7 10.0 %collective-permute-start.12 = (f32[3,2,66,66]{3,1,2,0:T(2,128)S(1)}, f32[3,2,66,66]{3,1,2,0:T(2,128)S(1)}, u32[]{:S(2)}, u32[]{:S(2)}) collective-permute-start(f32[3,2,66,66]{3,1,2,0:T(2,128)S(1)} %pad_maximum_fusion.5), channel_id=1, source_target_pairs={{1,0},{2,1},{3,2},{4,3},{5,4},{6,5},{7,6},{8,7},{9,8},{10,9},{11,1... | collective-permute-start | bytes 313640 | tf_op jit(solution)/shard_map/ppermute | solution.py:39
  306.6 3.1 collective-permute-start.13
  311.9 1.6 collective-permute-start.14
  (30 other events, 248.8 us)
where the time goes:
time: 324 us; the launch traced here: 318 us
  blocking collectives  108 us (33%)
  matrix products  91.1 us (28%)
  starting transfers between devices  42.6 us (13%)
  local copies, waits for them, and re-layouts  32.1 us (10%)
  other arithmetic  20.6 us (6%)
  waiting for transfers between devices  18.9 us (6%)
  between operations  5.41 us (2%)
    pmax x12, blocking collectives, by_axis(): return functools.reduce(lax.pmax, axes, value)  108 us
    dot_general x3, matrix products, scatter_tiles(): spread = jnp.einsum('bqn,bnm->qm', shaped, select_plane, precision=highest)  44.4 us
    dot_general x3, matrix products, tile_velocities(): gathered = jnp.einsum('qm,bnm->bqn', flat, select_plane, precision=highest)  36.4 us
    ppermute x6, starting transfers between devices, passed_along(): return lax.ppermute(value, axis, pairs)  33 us
    ppermute x6, waiting for transfers between devices, passed_along(): return lax.ppermute(value, axis, pairs)  13.5 us
    dot_general x4, local copies, waits for them, and re-layouts, scatter_tiles(): spread = jnp.einsum('bqn,bnm->qm', shaped, select_plane, precision=highest)  9.92 us
    mul x1, local copies, waits for them, and re-layouts, plane_selector(): joined = select_y[:, :, None, :, None] * select_z[:, None, :, None, :]  9.76 us
    ppermute x9, starting transfers between devices, swapped(): return lax.ppermute(value, axis, pairs)  9.56 us
  transfers between devices with their start and end apart: 15, of which 12 were waited for; matrix products, arithmetic and copies ran while one was open for 8% of the time, Pallas kernels for 0%

commit v1 on v0

v1 whole, which is shorter than its diff:
```python
import functools
import itertools

import jax
import jax.numpy as jnp
from jax import lax
from jax.experimental import pallas as pl
from jax.experimental.pallas import tpu as pltpu
from jax.sharding import PartitionSpec as P

STEPS = 3
LIVE = 4
PPB = 512
PARTICLES = LIVE * PPB
TILES = PARTICLES // 128
BIG = 3.4028235e38
FAR = 1e18
MESH = pl.DeviceIdType.MESH
F32 = jnp.float32
BF16 = jnp.bfloat16

mu_shear = 4.0
lame_first = 6.0
courant = 0.15
sound_speed = 3.7416573867739413
mass_floor = 0.05
gravity_x = 3.0
gravity_z = -9.0


def ring_distance(step):
    return min(step, 4 - step)


def peer_offsets():
    offsets = [o for o in itertools.product(range(4), range(4), range(4), range(2)) if any(o)]
    offsets.sort(key=lambda o: -(sum(ring_distance(c) for c in o[:3]) + 0.1 * o[3]))
    return offsets


def peer_at(me, offset):
    x, y, z, core = me // 32, me // 8 % 4, me // 2 % 4, me % 2
    x, y, z = (x + offset[0]) % 4, (y + offset[1]) % 4, (z + offset[2]) % 4
    return ((x * 4 + y) * 4 + z) * 2 + (core + offset[3]) % 2


PEERS = peer_offsets()


def halves(value):
    high = value.astype(BF16)
    return high, (value - high.astype(F32)).astype(BF16)


def spline(distance):
    magnitude = jnp.abs(distance)
    inner_part = 0.75 - magnitude * magnitude
    outer_part = 0.5 * (1.5 - magnitude) * (1.5 - magnitude)
    return jnp.where(magnitude < 0.5, inner_part, jnp.where(magnitude < 1.5, outer_part, 0.0))


def kirchhoff(f):
    determinant = (
        f[0] * (f[4] * f[8] - f[5] * f[7])
        - f[1] * (f[3] * f[8] - f[5] * f[6])
        + f[2] * (f[3] * f[7] - f[4] * f[6])
    )
    pressure = lame_first * (determinant - 1.0) * determinant
    stress = [None] * 9
    for r in range(3):
        for c in range(r, 3):
            product = f[3 * r] * f[3 * c] + f[3 * r + 1] * f[3 * c + 1] + f[3 * r + 2] * f[3 * c + 2]
            value = mu_shear * (product - 1.0) + pressure if r == c else mu_shear * product
            stress[3 * r + c] = stress[3 * c + r] = value
    return stress


def iota(shape, axis):
    return lax.broadcasted_iota(jnp.int32, shape, axis)


def kernel(
    pos, vel, dfm, aff, mass, vol, blk, live,
    o_d, o_v, o_f, o_c,
    pos_in, vel_in, dfm_in, aff_in, mass_in, vol_in,
    tile_a, tile_b, tile_c, coords, wx_t, wy_t, q_t, w_s, lh_s, part_s,
    select, low_s, high_s, blocks_own, blocks_got,
    top, got, from_prev, from_next,
    in_sem, top_send, top_recv, near_send, near_recv, blk_send, blk_recv,
):
    me = lax.axis_index("space")
    after = (me + 1) % 128
    before = (me + 127) % 128
    barrier = pltpu.get_barrier_semaphore()
    for offset in PEERS:
        pl.semaphore_signal(barrier, inc=1, device_id=(peer_at(me, offset),), device_id_type=MESH)

    columns = pl.ds(0, PARTICLES)
    loads = [
        pltpu.make_async_copy(vel.at[:, columns], vel_in, in_sem.at[0]),
        pltpu.make_async_copy(mass.at[pl.ds(0, TILES), :], mass_in, in_sem.at[1]),
        pltpu.make_async_copy(pos.at[:, columns], pos_in, in_sem.at[2]),
        pltpu.make_async_copy(dfm.at[:, columns], dfm_in, in_sem.at[3]),
        pltpu.make_async_copy(aff.at[:, columns], aff_in, in_sem.at[4]),
        pltpu.make_async_copy(vol.at[pl.ds(0, TILES), :], vol_in, in_sem.at[5]),
    ]
    for load in loads:
        load.start()

    alive = iota((TILES, 128), 0) // (TILES // LIVE) < live[0]
    by = [blk[b] // 16 for b in range(LIVE)]
    bz = [blk[b] % 16 for b in range(LIVE)]

    def per_bin(values, index):
        out = jnp.full(index.shape, values[LIVE - 1])
        for b in range(LIVE - 2, -1, -1):
            out = jnp.where(index == b, values[b], out)
        return out

    row_bin = iota((TILES, 128), 0) // (TILES // LIVE)
    anchor = [
        jnp.full((TILES, 128), 4 * me).astype(F32),
        (4 * per_bin(by, row_bin)).astype(F32),
        (4 * per_bin(bz, row_bin)).astype(F32),
    ]
    blocks_own[...] = per_bin([blk[b] for b in range(LIVE)], iota((8, 128), 0))

    def to_dense(source, rows, scratch, stride):
        for j in range(TILES):
            scratch[pl.ds(stride * j, rows), :] = source[:, pl.ds(128 * j, 128)]
        return [scratch[pl.ds(r, TILES, stride=stride), :] for r in range(rows)]

    loads[0].wait()
    loads[1].wait()
    v = to_dense(vel_in, 3, tile_a, 8)
    m = jnp.where(alive, mass_in[...], 0.0)

    def send_top(step, v):
        squared = jnp.where(m > 0.0, v[0] * v[0] + v[1] * v[1] + v[2] * v[2], 0.0)
        top[step] = jnp.max(squared, axis=0, keepdims=True)
        for k, offset in enumerate(PEERS):
            pltpu.make_async_remote_copy(
                top.at[step], got.at[step, k], top_send.at[step], top_recv.at[step],
                device_id=(peer_at(me, offset),), device_id_type=MESH,
            ).start()

    pl.semaphore_wait(barrier, len(PEERS))
    send_top(0, v)
    block_sends = []
    for side, target in enumerate((after, before)):
        copy = pltpu.make_async_remote_copy(
            blocks_own, blocks_got.at[side], blk_send.at[side], blk_recv.at[side],
            device_id=(target,), device_id_type=MESH,
        )
        copy.start()
        block_sends.append(copy)

    for load in loads[2:]:
        load.wait()
    x = to_dense(pos_in, 3, tile_b, 8)
    f = to_dense(dfm_in, 9, tile_c, 16)
    c = to_dense(aff_in, 9, tile_c, 16)
    volume = jnp.where(alive, vol_in[...], 0.0)
    travelled = [jnp.zeros((TILES, 128), F32)] * 3

    w_s[...] = jnp.zeros_like(w_s)
    q_t[...] = jnp.zeros_like(q_t)

    lane = iota((1, 128), 1)
    node_y = (lane % 64 // 8).astype(F32)
    node_z = (lane % 8).astype(F32)
    wide = iota((8, 512), 1)
    wide_bin = wide // 128
    node_j = 4 * per_bin(by, wide_bin) + wide % 64 // 8
    node_k = 4 * per_bin(bz, wide_bin) + wide % 8
    row = iota((8, 512), 0)
    for a in range(6):
        node_i = jnp.full((8, 512), 4 * me + a)
        lower = ((row == 0) & (node_i < 2)) | ((row == 1) & (node_j < 2)) | ((row == 2) & (node_k < 2))
        upper = ((row == 0) & (node_i >= 510)) | ((row == 1) & (node_j >= 64)) | ((row == 2) & (node_k >= 64))
        outside = (row > 2) | (node_i >= 512)
        low_s[pl.ds(8 * a, 8), :] = jnp.where(lower | outside, 0.0, -BIG)
        high_s[pl.ds(8 * a, 8), :] = jnp.where(upper | outside, 0.0, BIG)

    target_id = node_j[0:1] * 128 + node_k[0:1]

    def build_select(which, blocks_of, present):
        base = iota((64, 512), 0)
        base = base // 8 * 128 + base % 8
        for b in range(LIVE):
            block = blocks_of(b)
            source_id = base + (block // 16 * 512 + block % 16 * 4)
            same = (source_id == target_id) & present
            select[which, pl.ds(64 * b, 64), :] = jnp.where(same, 1.0, 0.0).astype(BF16)

    build_select(0, lambda b: blk[b], jnp.full((64, 512), me) >= 0)

    tile_row = iota((8, 128), 0)
    offsets = jnp.where(tile_row < 6, tile_row.astype(F32), FAR)
    left_half = lane < 64
    pair_low = tile_row < 4
    gravity = jnp.where(iota((8, 512), 0) == 0, gravity_x, jnp.where(iota((8, 512), 0) == 2, gravity_z, 0.0))
    node_y_wide = jnp.concatenate([node_y] * LIVE, axis=1)
    node_z_wide = jnp.concatenate([node_z] * LIVE, axis=1)
    left_wide = wide[0:1] % 128 < 64

    def wx_of(j, a):
        return jnp.broadcast_to(wx_t[pl.ds(8 * j + a, 1), :], (8, 128))

    near_sends = []
    for step in range(STEPS):
        local = [x[i] - anchor[i] for i in range(3)]
        for i in range(3):
            coords[i] = local[i]
        stress = kirchhoff(f)
        scaled = -4.0 * volume
        for o in range(3):
            affine_m = [m * c[3 * o + i] for i in range(3)]
            affine_s = [scaled * stress[3 * o + i] for i in range(3)]
            base_m = m * v[o]
            for i in range(3):
                base_m = base_m - affine_m[i] * local[i]
            base_s = -(affine_s[0] * local[0] + affine_s[1] * local[1] + affine_s[2] * local[2])
            q_t[0, pl.ds(o, TILES, stride=8), :] = base_m
            q_t[0, pl.ds(4 + o, TILES, stride=8), :] = base_s
            for i in range(3):
                q_t[1 + i, pl.ds(o, TILES, stride=8), :] = affine_m[i]
                q_t[1 + i, pl.ds(4 + o, TILES, stride=8), :] = affine_s[i]
        q_t[0, pl.ds(3, TILES, stride=8), :] = m

        for j in range(TILES):
            b, part = j // 4, pl.ds(128 * (j % 4), 128)
            here = pl.ds(8 * j, 8)
            near = [jnp.broadcast_to(coords[i, pl.ds(j, 1), :], (8, 128)) for i in range(3)]
            wx_t[here, :] = spline(offsets - near[0])
            wy_t[here, :] = spline(offsets - near[1])
            wz = spline(offsets - near[2])
            wyz = jnp.concatenate(
                [jnp.broadcast_to(wy_t[pl.ds(8 * j + a, 1), :], (8, 128)) * wz for a in range(6)], axis=0
            )
            high, low = halves(wyz)
            w_s[b, 0:48, part] = high
            w_s[b, 64:112, part] = high
            w_s[b, 128:176, part] = low
            w_s[b, 192:240, part] = low
            weights = [wx_of(j, a) for a in range(6)]
            q = [q_t[g, here, :] for g in range(4)]
            rows = [weights[a] * (q[0] + float(a) * q[1] if a else q[0]) for a in range(6)]
            rows += [weights[a] * q[2] for a in range(6)]
            rows += [weights[a] * q[3] for a in range(6)]
            high, low = halves(jnp.concatenate(rows, axis=0))
            lh_s[0:144, pl.ds(128 * j, 128)] = high
            lh_s[144:288, pl.ds(128 * j, 128)] = low

        totals = []
        for b in range(LIVE):
            summed = lax.dot_general(
                lh_s[:, pl.ds(PPB * b, PPB)], w_s[b], (((1,), (1,)), ((), ())), preferred_element_type=F32
            )
            totals.append(summed[0:144, 0:128] + summed[0:144, 128:256] + summed[144:288, 0:128])
        for h in range(2):
            both = jnp.where(left_half, totals[2 * h], totals[2 * h + 1])
            part_s[step, :, pl.ds(128 * h, 128)] = both[0:48] + node_y * both[48:96] + node_z * both[96:144]

        sends = [
            pltpu.make_async_remote_copy(
                part_s.at[step, pl.ds(32, 16), :], from_prev.at[step],
                near_send.at[step, 0], near_recv.at[step, 0], device_id=(after,), device_id_type=MESH,
            ),
            pltpu.make_async_remote_copy(
                part_s.at[step, pl.ds(0, 16), :], from_next.at[step],
                near_send.at[step, 1], near_recv.at[step, 1], device_id=(before,), device_id_type=MESH,
            ),
        ]
        for send in sends:
            send.start()
        near_sends += sends

        def merged(value, which):
            high, low = halves(value)
            spread = jnp.dot(
                jnp.concatenate([high, low], axis=0), select[which], preferred_element_type=F32
            )
            return spread[: value.shape[0]] + spread[value.shape[0] :]

        own = merged(part_s[step], 0)
        if step == 0:
            for copy in block_sends:
                copy.wait_recv()
            no_prev = jnp.full((64, 512), me) > 0
            no_next = jnp.full((64, 512), me) < 127
            build_select(1, lambda b: jnp.concatenate([blocks_got[0, pl.ds(b, 1), :]] * 4, axis=1), no_prev)
            build_select(2, lambda b: jnp.concatenate([blocks_got[1, pl.ds(b, 1), :]] * 4, axis=1), no_next)
        for send in sends:
            send.wait_recv()
        lower_planes = merged(from_prev[step], 1)
        upper_planes = merged(from_next[step], 2)
        planes = [own[8 * a : 8 * a + 8] for a in range(6)]
        for k in range(2):
            planes[k] = planes[k] + lower_planes[8 * k : 8 * k + 8]
            planes[4 + k] = planes[4 + k] + upper_planes[8 * k : 8 * k + 8]

        pltpu.make_async_copy(got.at[step], got.at[step], top_recv.at[step]).wait()
        fastest = jnp.maximum(top[step], jnp.max(got[step], axis=0))
        fastest = jnp.max(fastest, axis=1, keepdims=True)
        dt = courant / (jnp.sqrt(fastest) + sound_speed)

        node_rows, moments = [], []
        for a in range(6):
            here = pl.ds(8 * a, 8)
            node_mass = jnp.maximum(planes[a][3:4], mass_floor)
            momentum = planes[a] + dt * pltpu.roll(planes[a], 4, 0)
            g = momentum / node_mass + dt * gravity
            g = jnp.minimum(jnp.maximum(g, low_s[here, :]), high_s[here, :])
            node_rows.append(g + pltpu.roll(g * node_y_wide, 4, 0))
            moments.append(g * node_z_wide)
        for k in range(3):
            node_rows.append(moments[2 * k] + pltpu.roll(moments[2 * k + 1], 4, 0))
        nodes = jnp.concatenate(node_rows, axis=0)
        rounded = nodes.astype(BF16).astype(F32)
        stacked = jnp.where(left_wide, rounded, nodes - rounded).astype(BF16)

        for b in range(LIVE):
            own_nodes = stacked[:, 128 * b : 128 * b + 128]
            spread = jnp.dot(
                jnp.concatenate([own_nodes, own_nodes], axis=1), w_s[b], preferred_element_type=F32
            )
            for k in range(4):
                j = 4 * b + k
                here = pl.ds(8 * j, 8)
                t = [spread[8 * a : 8 * a + 8, 128 * k : 128 * k + 128] for a in range(9)]
                weights = [wx_of(j, a) for a in range(6)]
                terms = [weights[a] * t[a] for a in range(6)]
                plain = terms[0] + terms[1] + terms[2] + terms[3] + terms[4] + terms[5]
                first = terms[1] + 2.0 * terms[2] + 3.0 * terms[3] + 4.0 * terms[4] + 5.0 * terms[5]
                third = [
                    jnp.where(pair_low, weights[2 * h], weights[2 * h + 1]) * t[6 + h] for h in range(3)
                ]
                third = third[0] + third[1] + third[2]
                tile_a[here, :] = plain
                tile_b[here, :] = first
                tile_c[here, :] = third + pltpu.roll(third, 4, 0)

        v = [tile_a[pl.ds(o, TILES, stride=8), :] for o in range(3)]
        if step + 1 < STEPS:
            send_top(step + 1, v)
        moment = [
            [tile_b[pl.ds(o, TILES, stride=8), :] for o in range(3)],
            [tile_a[pl.ds(4 + o, TILES, stride=8), :] for o in range(3)],
            [tile_c[pl.ds(o, TILES, stride=8), :] for o in range(3)],
        ]
        c = [4.0 * (moment[i][o] - v[o] * local[i]) for o in range(3) for i in range(3)]
        f = [
            f[3 * r + s]
            + dt * (c[3 * r] * f[s] + c[3 * r + 1] * f[3 + s] + c[3 * r + 2] * f[6 + s])
            for r in range(3)
            for s in range(3)
        ]
        moved = [dt * v[i] for i in range(3)]
        x = [x[i] + moved[i] for i in range(3)]
        travelled = [travelled[i] + moved[i] for i in range(3)]

    for output, values in ((o_d, travelled), (o_v, v), (o_f, f), (o_c, c)):
        rows = len(values)
        stride = 8 if rows == 3 else 16
        scratch = tile_a if rows == 3 else tile_c
        for r in range(rows):
            scratch[pl.ds(r, TILES, stride=stride), :] = jnp.where(alive, values[r], 0.0)
        for j in range(TILES):
            output[:, pl.ds(128 * j, 128)] = scratch[pl.ds(stride * j, rows), :]
        output[:, pl.ds(PARTICLES, PARTICLES)] = jnp.zeros((rows, PARTICLES), F32)

    for send in near_sends + block_sends:
        send.wait_send()
    for step in range(STEPS):
        pltpu.make_async_copy(got.at[step], got.at[step], top_send.at[step]).wait()


def local(positions, velocity, deformation, affine, particle_mass, volume, bin_block, live_count):
    total = positions.shape[1]
    hbm = pl.BlockSpec(memory_space=pl.ANY)
    smem = pl.BlockSpec(memory_space=pltpu.SMEM)
    vmem = pl.BlockSpec(memory_space=pltpu.VMEM)
    return pl.pallas_call(
        kernel,
        out_shape=[jax.ShapeDtypeStruct((rows, total), F32) for rows in (3, 3, 9, 9)],
        in_specs=[hbm] * 6 + [smem] * 2,
        out_specs=[vmem] * 4,
        scratch_shapes=[
            pltpu.VMEM((3, PARTICLES), F32),
            pltpu.VMEM((3, PARTICLES), F32),
            pltpu.VMEM((9, PARTICLES), F32),
            pltpu.VMEM((9, PARTICLES), F32),
            pltpu.VMEM((TILES, 128), F32),
            pltpu.VMEM((TILES, 128), F32),
            pltpu.VMEM((8 * TILES, 128), F32),
            pltpu.VMEM((8 * TILES, 128), F32),
            pltpu.VMEM((16 * TILES, 128), F32),
            pltpu.VMEM((3, TILES, 128), F32),
            pltpu.VMEM((8 * TILES, 128), F32),
            pltpu.VMEM((8 * TILES, 128), F32),
            pltpu.VMEM((4, 8 * TILES, 128), F32),
            pltpu.VMEM((LIVE, 256, PPB), BF16),
            pltpu.VMEM((288, PARTICLES), BF16),
            pltpu.VMEM((STEPS, 48, 256), F32),
            pltpu.VMEM((3, 256, 512), BF16),
            pltpu.VMEM((48, 512), F32),
            pltpu.VMEM((48, 512), F32),
            pltpu.VMEM((8, 128), jnp.int32),
            pltpu.VMEM((2, 8, 128), jnp.int32),
            pltpu.VMEM((STEPS, 1, 128), F32),
            pltpu.VMEM((STEPS, len(PEERS), 1, 128), F32),
            pltpu.VMEM((STEPS, 16, 256), F32),
            pltpu.VMEM((STEPS, 16, 256), F32),
            pltpu.SemaphoreType.DMA((6,)),
            pltpu.SemaphoreType.DMA((STEPS,)),
            pltpu.SemaphoreType.DMA((STEPS,)),
            pltpu.SemaphoreType.DMA((STEPS, 2)),
            pltpu.SemaphoreType.DMA((STEPS, 2)),
            pltpu.SemaphoreType.DMA((2,)),
            pltpu.SemaphoreType.DMA((2,)),
        ],
        compiler_params=pltpu.CompilerParams(collective_id=0, has_side_effects=True),
        name="material_points",
    )(
        positions, velocity, deformation, affine,
        particle_mass.reshape(-1, 128), volume.reshape(-1, 128), bin_block, live_count,
    )


def solution(mesh):
    wide, flat = P(None, "space"), P("space")
    return jax.shard_map(
        local,
        mesh=mesh,
        in_specs=(wide,) * 4 + (flat,) * 4,
        out_specs=(wide,) * 4,
        check_vma=False,
    )
```

time: 324 us -> 38.1 us (0.12)
  the two profiles are of different devices: /device:TPU:3 before, /device:TPU:0 now
where the time goes in v1:
time: 38.1 us; the launch traced here: 37.9 us
  Pallas kernels  31.9 us (84%)
  local copies, waits for them, and re-layouts  4.75 us (12%)
  between operations  1.3 us (3%)
    pallas_call x1, Pallas kernels, local(): pl.pallas_call(kernel, out_shape=[jax.ShapeDtypeStruct((rows, total), F32...  31.9 us
    unnamed x8, local copies, waits for them, and re-layouts  4.75 us

profile of v1, /device:TPU:0, one launch (start us, length us, event | category | flops | bytes accessed | tf_op | source)
XLA Modules:
  0.0 37.9 jit_solution(17272608792460811782)
XLA Ops:
  1.3 31.9 %material_points.1 = (f32[3,4096]{1,0:T(4,128)}, f32[3,4096]{1,0:T(4,128)}, f32[9,4096]{1,0:T(8,128)}, f32[9,4096]{1,0:T(8,128)}) custom-call(f32[3,4096]{1,0:T(4,128)} %pos.1, f32[3,4096]{1,0:T(4,128)} %vel.1, f32[9,4096]{1,0:T(8,128)} %dfm.1, f32[9,4096]{1,0:T(8,128)} %aff.1, f32[32,128]{1,0:T(8,128)} %bitcast.2, f32[32,128]{1,0:T(8,128)} %bitcast.3, ...), custom_call_target="tpu_custom_call" | custom-call | tf_op jit(solution)/shard_map/material_points/pallas_call | solution.py:384
  33.1 0.0 copy-start.1
  33.1 1.5 %copy.17 = f32[3,4096]{1,0:T(4,128)} copy(f32[3,4096]{1,0:T(4,128)} %get-tuple-element.8) | data formatting | bytes 98304
  34.7 1.5 %copy.18 = f32[3,4096]{1,0:T(4,128)} copy(f32[3,4096]{1,0:T(4,128)} %get-tuple-element.9) | data formatting | bytes 98304
  36.2 0.0 copy-done.1
  36.2 0.0 copy-start
  36.2 0.7 %copy.19 = f32[9,4096]{1,0:T(8,128)} copy(f32[9,4096]{1,0:T(8,128)S(1)} %copy-done.1) | data formatting | bytes 294912
  36.9 0.3 copy-done
  37.2 0.7 %copy.20 = f32[9,4096]{1,0:T(8,128)} copy(f32[9,4096]{1,0:T(8,128)S(1)} %copy-done) | data formatting | bytes 294912
Async XLA Ops:
  33.1 3.0 %copy-start.1 = (f32[9,4096]{1,0:T(8,128)S(1)}, f32[9,4096]{1,0:T(8,128)}, u32[]{:S(2)}) copy-start(f32[9,4096]{1,0:T(8,128)} %get-tuple-element.10) | copy-start | bytes 442372
  36.2 1.0 %copy-start = (f32[9,4096]{1,0:T(8,128)S(1)}, f32[9,4096]{1,0:T(8,128)}, u32[]{:S(2)}) copy-start(f32[9,4096]{1,0:T(8,128)} %get-tuple-element.11) | copy-start | bytes 442372

commit v2 on v1

--- a/solution.py
+++ b/solution.py
@@ -80,9 +80,9 @@
 
 
 def kernel(
-    pos, vel, dfm, aff, mass, vol, blk, live,
+    pos, vel, dfm, aff, mass, vol, blk_hbm, live_hbm,
     o_d, o_v, o_f, o_c,
-    pos_in, vel_in, dfm_in, aff_in, mass_in, vol_in,
+    blk, live, pos_in, vel_in, dfm_in, aff_in, mass_in, vol_in,
     tile_a, tile_b, tile_c, coords, wx_t, wy_t, q_t, w_s, lh_s, part_s,
     select, low_s, high_s, blocks_own, blocks_got,
     top, got, from_prev, from_next,
@@ -98,7 +98,9 @@
     columns = pl.ds(0, PARTICLES)
     loads = [
         pltpu.make_async_copy(vel.at[:, columns], vel_in, in_sem.at[0]),
+        pltpu.make_async_copy(live_hbm, live, in_sem.at[7]),
         pltpu.make_async_copy(mass.at[pl.ds(0, TILES), :], mass_in, in_sem.at[1]),
+        pltpu.make_async_copy(blk_hbm, blk, in_sem.at[6]),
         pltpu.make_async_copy(pos.at[:, columns], pos_in, in_sem.at[2]),
         pltpu.make_async_copy(dfm.at[:, columns], dfm_in, in_sem.at[3]),
         pltpu.make_async_copy(aff.at[:, columns], aff_in, in_sem.at[4]),
@@ -107,31 +109,14 @@
     for load in loads:
         load.start()
 
-    alive = iota((TILES, 128), 0) // (TILES // LIVE) < live[0]
-    by = [blk[b] // 16 for b in range(LIVE)]
-    bz = [blk[b] % 16 for b in range(LIVE)]
-
-    def per_bin(values, index):
-        out = jnp.full(index.shape, values[LIVE - 1])
-        for b in range(LIVE - 2, -1, -1):
-            out = jnp.where(index == b, values[b], out)
-        return out
-
-    row_bin = iota((TILES, 128), 0) // (TILES // LIVE)
-    anchor = [
-        jnp.full((TILES, 128), 4 * me).astype(F32),
-        (4 * per_bin(by, row_bin)).astype(F32),
-        (4 * per_bin(bz, row_bin)).astype(F32),
-    ]
-    blocks_own[...] = per_bin([blk[b] for b in range(LIVE)], iota((8, 128), 0))
-
     def to_dense(source, rows, scratch, stride):
         for j in range(TILES):
             scratch[pl.ds(stride * j, rows), :] = source[:, pl.ds(128 * j, 128)]
         return [scratch[pl.ds(r, TILES, stride=stride), :] for r in range(rows)]
 
-    loads[0].wait()
-    loads[1].wait()
+    for load in loads[:3]:
+        load.wait()
+    alive = iota((TILES, 128), 0) // (TILES // LIVE) < live[0, 0]
     v = to_dense(vel_in, 3, tile_a, 8)
     m = jnp.where(alive, mass_in[...], 0.0)
 
@@ -146,6 +131,24 @@
 
     pl.semaphore_wait(barrier, len(PEERS))
     send_top(0, v)
+    loads[3].wait()
+    by = [blk[b] // 16 for b in range(LIVE)]
+    bz = [blk[b] % 16 for b in range(LIVE)]
+
+    def per_bin(values, index):
+        out = jnp.full(index.shape, values[LIVE - 1])
+        for b in range(LIVE - 2, -1, -1):
+            out = jnp.where(index == b, values[b], out)
+        return out
+
+    row_bin = iota((TILES, 128), 0) // (TILES // LIVE)
+    anchor = [
+        jnp.full((TILES, 128), 4 * me).astype(F32),
+        (4 * per_bin(by, row_bin)).astype(F32),
+        (4 * per_bin(bz, row_bin)).astype(F32),
+    ]
+    blocks_own[...] = per_bin([blk[b] for b in range(LIVE)], iota((8, 128), 0))
+
     block_sends = []
     for side, target in enumerate((after, before)):
         copy = pltpu.make_async_remote_copy(
@@ -155,7 +158,7 @@
         copy.start()
         block_sends.append(copy)
 
-    for load in loads[2:]:
+    for load in loads[4:]:
         load.wait()
     x = to_dense(pos_in, 3, tile_b, 8)
     f = to_dense(dfm_in, 9, tile_c, 16)
@@ -368,7 +371,6 @@
             scratch[pl.ds(r, TILES, stride=stride), :] = jnp.where(alive, values[r], 0.0)
         for j in range(TILES):
             output[:, pl.ds(128 * j, 128)] = scratch[pl.ds(stride * j, rows), :]
-        output[:, pl.ds(PARTICLES, PARTICLES)] = jnp.zeros((rows, PARTICLES), F32)
 
     for send in near_sends + block_sends:
         send.wait_send()
@@ -376,17 +378,34 @@
         pltpu.make_async_copy(got.at[step], got.at[step], top_send.at[step]).wait()
 
 
+def spread_out(d, v, f, c, o_d, o_v, o_f, o_c, nothing, sems):
+    nothing[...] = jnp.zeros_like(nothing)
+    copies = []
+    for k, (source, target) in enumerate(((d, o_d), (v, o_v), (f, o_f), (c, o_c))):
+        rows = source.shape[0]
+        empty = nothing if rows == 9 else nothing.at[pl.ds(0, rows), :]
+        copies.append(pltpu.make_async_copy(source, target.at[:, pl.ds(0, PARTICLES)], sems.at[2 * k]))
+        copies.append(
+            pltpu.make_async_copy(empty, target.at[:, pl.ds(PARTICLES, PARTICLES)], sems.at[2 * k + 1])
+        )
+    for copy in copies:
+        copy.start()
+    for copy in copies:
+        copy.wait()
+
+
 def local(positions, velocity, deformation, affine, particle_mass, volume, bin_block, live_count):
     total = positions.shape[1]
     hbm = pl.BlockSpec(memory_space=pl.ANY)
-    smem = pl.BlockSpec(memory_space=pltpu.SMEM)
     vmem = pl.BlockSpec(memory_space=pltpu.VMEM)
-    return pl.pallas_call(
+    results = pl.pallas_call(
         kernel,
-        out_shape=[jax.ShapeDtypeStruct((rows, total), F32) for rows in (3, 3, 9, 9)],
-        in_specs=[hbm] * 6 + [smem] * 2,
+        out_shape=[pltpu.VMEM((rows, PARTICLES), F32) for rows in (3, 3, 9, 9)],
+        in_specs=[hbm] * 8,
         out_specs=[vmem] * 4,
         scratch_shapes=[
+            pltpu.SMEM((8,), jnp.int32),
+            pltpu.SMEM((1, 1), jnp.int32),
             pltpu.VMEM((3, PARTICLES), F32),
             pltpu.VMEM((3, PARTICLES), F32),
             pltpu.VMEM((9, PARTICLES), F32),
@@ -412,7 +431,7 @@
             pltpu.VMEM((STEPS, len(PEERS), 1, 128), F32),
             pltpu.VMEM((STEPS, 16, 256), F32),
             pltpu.VMEM((STEPS, 16, 256), F32),
-            pltpu.SemaphoreType.DMA((6,)),
+            pltpu.SemaphoreType.DMA((8,)),
             pltpu.SemaphoreType.DMA((STEPS,)),
             pltpu.SemaphoreType.DMA((STEPS,)),
             pltpu.SemaphoreType.DMA((STEPS, 2)),
@@ -424,8 +443,17 @@
         name="material_points",
     )(
         positions, velocity, deformation, affine,
-        particle_mass.reshape(-1, 128), volume.reshape(-1, 128), bin_block, live_count,
+        particle_mass.reshape(-1, 128), volume.reshape(-1, 128), bin_block,
+        live_count.reshape(1, 1),
     )
+    return pl.pallas_call(
+        spread_out,
+        out_shape=[jax.ShapeDtypeStruct((rows, total), F32) for rows in (3, 3, 9, 9)],
+        in_specs=[vmem] * 4,
+        out_specs=[hbm] * 4,
+        scratch_shapes=[pltpu.VMEM((9, PARTICLES), F32), pltpu.SemaphoreType.DMA((8,))],
+        name="spread_out",
+    )(*(pltpu.with_memory_space_constraint(result, pltpu.VMEM) for result in results))
 
 
 def solution(mesh):

time: 38.1 us -> 32.7 us (0.86)
  local copies, waits for them, and re-layouts: 4.75 us -> 0 us
  Pallas kernels: 31.9 us -> 31.3 us
    unnamed x8 -> x0, local copies, waits for them, and re-layouts: 4.75 us -> none
    pallas_call x1 -> x2, Pallas kernels: 31.9 us -> 31.3 us  [the longest x1 30.4 us: local(): pl.pallas_call(kernel, out_shape=[pltpu.VMEM((rows, PARTICLES), F32) for...]
where the time goes in v2:
time: 32.7 us; the launch traced here: 32.6 us
  Pallas kernels  31.3 us (96%)
  between operations  1.29 us (4%)
    pallas_call x1, Pallas kernels, local(): pl.pallas_call(kernel, out_shape=[pltpu.VMEM((rows, PARTICLES), F32) for...  30.4 us
    pallas_call x1, Pallas kernels, local(): pl.pallas_call(spread_out, out_shape=[jax.ShapeDtypeStruct((rows, total),...  0.9 us

profile of v2, /device:TPU:0, one launch (start us, length us, event | category | flops | bytes accessed | tf_op | source)
XLA Modules:
  0.0 32.6 jit_solution(11757787673549811030)
XLA Ops:
  1.3 30.4 %material_points.1 = (f32[3,2048]{1,0:T(4,128)S(1)}, f32[3,2048]{1,0:T(4,128)S(1)}, f32[9,2048]{1,0:T(8,128)S(1)}, f32[9,2048]{1,0:T(8,128)S(1)}) custom-call(f32[3,4096]{1,0:T(4,128)} %pos.1, f32[3,4096]{1,0:T(4,128)} %vel.1, f32[9,4096]{1,0:T(8,128)} %dfm.1, f32[9,4096]{1,0:T(8,128)} %aff.1, f32[32,128]{1,0:T(8,128)} %bitcast.4, f32[32,128]{1,0:T(8,128)} %bitcast.5, ...), custom_call_target="tpu_custom_call" | custom-call | tf_op jit(solution)/shard_map/material_points/pallas_call | solution.py:401
  31.7 0.9 %spread_out.1 = (f32[3,4096]{1,0:T(4,128)}, f32[3,4096]{1,0:T(4,128)}, f32[9,4096]{1,0:T(8,128)}, f32[9,4096]{1,0:T(8,128)}) custom-call(f32[3,2048]{1,0:T(4,128)S(1)} %get-tuple-element.8.d, f32[3,2048]{1,0:T(4,128)S(1)} %get-tuple-element.9.v, f32[9,2048]{1,0:T(8,128)S(1)} %get-tuple-element.10.f, f32[9,2048]{1,0:T(8,128)S(1)} %get-tuple-element.11.c), custom_call_target="tpu_custom_call" | custom-call | tf_op jit(solution)/shard_map/spread_out/pallas_call | solution.py:449

commit v3 on v2

--- a/solution.py
+++ b/solution.py
@@ -38,10 +38,13 @@
     return offsets
 
 
-def peer_at(me, offset):
+def peer_ids(me):
     x, y, z, core = me // 32, me // 8 % 4, me // 2 % 4, me % 2
-    x, y, z = (x + offset[0]) % 4, (y + offset[1]) % 4, (z + offset[2]) % 4
-    return ((x * 4 + y) * 4 + z) * 2 + (core + offset[3]) % 2
+    outer = [
+        [(x + dx) % 4 * 32 + (y + dy) % 4 * 8 for dy in range(4)] for dx in range(4)
+    ]
+    inner = [[(z + dz) % 4 * 2 + (core + dc) % 2 for dc in range(2)] for dz in range(4)]
+    return [outer[dx][dy] + inner[dz][dc] for dx, dy, dz, dc in PEERS]
 
 
 PEERS = peer_offsets()
@@ -91,10 +94,6 @@
     me = lax.axis_index("space")
     after = (me + 1) % 128
     before = (me + 127) % 128
-    barrier = pltpu.get_barrier_semaphore()
-    for offset in PEERS:
-        pl.semaphore_signal(barrier, inc=1, device_id=(peer_at(me, offset),), device_id_type=MESH)
-
     columns = pl.ds(0, PARTICLES)
     loads = [
         pltpu.make_async_copy(vel.at[:, columns], vel_in, in_sem.at[0]),
@@ -109,6 +108,11 @@
     for load in loads:
         load.start()
 
+    barrier = pltpu.get_barrier_semaphore()
+    peers = peer_ids(me)
+    for peer in peers:
+        pl.semaphore_signal(barrier, inc=1, device_id=(peer,), device_id_type=MESH)
+
     def to_dense(source, rows, scratch, stride):
         for j in range(TILES):
             scratch[pl.ds(stride * j, rows), :] = source[:, pl.ds(128 * j, 128)]
@@ -120,17 +124,20 @@
     v = to_dense(vel_in, 3, tile_a, 8)
     m = jnp.where(alive, mass_in[...], 0.0)
 
-    def send_top(step, v):
+    def find_top(step, v):
         squared = jnp.where(m > 0.0, v[0] * v[0] + v[1] * v[1] + v[2] * v[2], 0.0)
         top[step] = jnp.max(squared, axis=0, keepdims=True)
-        for k, offset in enumerate(PEERS):
+
+    def send_top(step):
+        for k, peer in enumerate(peers):
             pltpu.make_async_remote_copy(
                 top.at[step], got.at[step, k], top_send.at[step], top_recv.at[step],
-                device_id=(peer_at(me, offset),), device_id_type=MESH,
+                device_id=(peer,), device_id_type=MESH,
             ).start()
 
     pl.semaphore_wait(barrier, len(PEERS))
-    send_top(0, v)
+    find_top(0, v)
+    send_top(0)
     loads[3].wait()
     by = [blk[b] // 16 for b in range(LIVE)]
     bz = [blk[b] % 16 for b in range(LIVE)]
@@ -149,14 +156,33 @@
     ]
     blocks_own[...] = per_bin([blk[b] for b in range(LIVE)], iota((8, 128), 0))
 
+
+    def start_near(pair):
+        pl.when(me < 127)(pair[0].start)
+        pl.when(me > 0)(pair[1].start)
+
+    def wait_near(pair):
+        pl.when(me > 0)(pair[0].wait_recv)
+        pl.when(me < 127)(pair[1].wait_recv)
+
+    @pl.when(me == 0)
+    def _():
+        from_prev[...] = jnp.zeros_like(from_prev)
+        blocks_got[0] = jnp.zeros_like(blocks_own)
+
+    @pl.when(me == 127)
+    def _():
+        from_next[...] = jnp.zeros_like(from_next)
+        blocks_got[1] = jnp.zeros_like(blocks_own)
+
     block_sends = []
     for side, target in enumerate((after, before)):
         copy = pltpu.make_async_remote_copy(
             blocks_own, blocks_got.at[side], blk_send.at[side], blk_recv.at[side],
             device_id=(target,), device_id_type=MESH,
         )
-        copy.start()
         block_sends.append(copy)
+    start_near(block_sends)
 
     for load in loads[4:]:
         load.wait()
@@ -275,9 +301,8 @@
                 near_send.at[step, 1], near_recv.at[step, 1], device_id=(before,), device_id_type=MESH,
             ),
         ]
-        for send in sends:
-            send.start()
-        near_sends += sends
+        start_near(sends)
+        near_sends.append(sends)
 
         def merged(value, which):
             high, low = halves(value)
@@ -288,14 +313,12 @@
 
         own = merged(part_s[step], 0)
         if step == 0:
-            for copy in block_sends:
-                copy.wait_recv()
+            wait_near(block_sends)
             no_prev = jnp.full((64, 512), me) > 0
             no_next = jnp.full((64, 512), me) < 127
             build_select(1, lambda b: jnp.concatenate([blocks_got[0, pl.ds(b, 1), :]] * 4, axis=1), no_prev)
             build_select(2, lambda b: jnp.concatenate([blocks_got[1, pl.ds(b, 1), :]] * 4, axis=1), no_next)
-        for send in sends:
-            send.wait_recv()
+        wait_near(sends)
         lower_planes = merged(from_prev[step], 1)
         upper_planes = merged(from_next[step], 2)
         planes = [own[8 * a : 8 * a + 8] for a in range(6)]
@@ -346,7 +369,8 @@
 
         v = [tile_a[pl.ds(o, TILES, stride=8), :] for o in range(3)]
         if step + 1 < STEPS:
-            send_top(step + 1, v)
+            find_top(step + 1, v)
+            send_top(step + 1)
         moment = [
             [tile_b[pl.ds(o, TILES, stride=8), :] for o in range(3)],
             [tile_a[pl.ds(4 + o, TILES, stride=8), :] for o in range(3)],
@@ -372,8 +396,9 @@
         for j in range(TILES):
             output[:, pl.ds(128 * j, 128)] = scratch[pl.ds(stride * j, rows), :]
 
-    for send in near_sends + block_sends:
-        send.wait_send()
+    for pair in near_sends + [block_sends]:
+        pl.when(me < 127)(pair[0].wait_send)
+        pl.when(me > 0)(pair[1].wait_send)
     for step in range(STEPS):
         pltpu.make_async_copy(got.at[step], got.at[step], top_send.at[step]).wait()
 

time: 32.7 us -> 31.4 us (0.960)
  the two profiles are of different devices: /device:TPU:0 before, /device:TPU:1 now
where the time goes in v3:
time: 31.4 us; the launch traced here: 31.3 us
  Pallas kernels  30 us (96%)
  between operations  1.29 us (4%)
    pallas_call x1, Pallas kernels, local(): pl.pallas_call(kernel, out_shape=[pltpu.VMEM((rows, PARTICLES), F32) for...  29.1 us
    pallas_call x1, Pallas kernels, local(): pl.pallas_call(spread_out, out_shape=[jax.ShapeDtypeStruct((rows, total),...  0.9 us

profile of v3, /device:TPU:1, one launch (start us, length us, event | category | flops | bytes accessed | tf_op | source)
XLA Modules:
  0.0 31.3 jit_solution(8836614073664722040)
XLA Ops:
  1.3 29.1 %material_points.1 = (f32[3,2048]{1,0:T(4,128)S(1)}, f32[3,2048]{1,0:T(4,128)S(1)}, f32[9,2048]{1,0:T(8,128)S(1)}, f32[9,2048]{1,0:T(8,128)S(1)}) custom-call(f32[3,4096]{1,0:T(4,128)} %pos.1, f32[3,4096]{1,0:T(4,128)} %vel.1, f32[9,4096]{1,0:T(8,128)} %dfm.1, f32[9,4096]{1,0:T(8,128)} %aff.1, f32[32,128]{1,0:T(8,128)} %bitcast.4, f32[32,128]{1,0:T(8,128)} %bitcast.5, ...), custom_call_target="tpu_custom_call" | custom-call | tf_op jit(solution)/shard_map/material_points/pallas_call | solution.py:426
  30.4 0.9 %spread_out.1 = (f32[3,4096]{1,0:T(4,128)}, f32[3,4096]{1,0:T(4,128)}, f32[9,4096]{1,0:T(8,128)}, f32[9,4096]{1,0:T(8,128)}) custom-call(f32[3,2048]{1,0:T(4,128)S(1)} %get-tuple-element.8.d, f32[3,2048]{1,0:T(4,128)S(1)} %get-tuple-element.9.v, f32[9,2048]{1,0:T(8,128)S(1)} %get-tuple-element.10.f, f32[9,2048]{1,0:T(8,128)S(1)} %get-tuple-element.11.c), custom_call_target="tpu_custom_call" | custom-call | tf_op jit(solution)/shard_map/spread_out/pallas_call | solution.py:474

commit v4 on v3

--- a/solution.py
+++ b/solution.py
@@ -44,10 +44,12 @@
         [(x + dx) % 4 * 32 + (y + dy) % 4 * 8 for dy in range(4)] for dx in range(4)
     ]
     inner = [[(z + dz) % 4 * 2 + (core + dc) % 2 for dc in range(2)] for dz in range(4)]
-    return [outer[dx][dy] + inner[dz][dc] for dx, dy, dz, dc in PEERS]
+    return (outer[dx][dy] + inner[dz][dc] for dx, dy, dz, dc in PEERS)
 
 
 PEERS = peer_offsets()
+SHARED_PLANES = (0, 1, 4, 5)
+INNER_PLANES = (2, 3)
 
 
 def halves(value):
@@ -86,7 +88,7 @@
     pos, vel, dfm, aff, mass, vol, blk_hbm, live_hbm,
     o_d, o_v, o_f, o_c,
     blk, live, pos_in, vel_in, dfm_in, aff_in, mass_in, vol_in,
-    tile_a, tile_b, tile_c, coords, wx_t, wy_t, q_t, w_s, lh_s, part_s,
+    tile_a, tile_b, tile_c, coords, wx_t, wy_t, q_t, w_s, lh_s, lh_inner, part_s,
     select, low_s, high_s, blocks_own, blocks_got,
     top, got, from_prev, from_next,
     in_sem, top_send, top_recv, near_send, near_recv, blk_send, blk_recv,
@@ -109,8 +111,9 @@
         load.start()
 
     barrier = pltpu.get_barrier_semaphore()
-    peers = peer_ids(me)
-    for peer in peers:
+    peers = []
+    for peer in peer_ids(me):
+        peers.append(peer)
         pl.semaphore_signal(barrier, inc=1, device_id=(peer,), device_id_type=MESH)
 
     def to_dense(source, rows, scratch, stride):
@@ -257,6 +260,34 @@
                 q_t[1 + i, pl.ds(4 + o, TILES, stride=8), :] = affine_s[i]
         q_t[0, pl.ds(3, TILES, stride=8), :] = m
 
+        def fill(j, planes, target):
+            here, count = pl.ds(8 * j, 8), 24 * len(planes)
+            weights = {a: wx_of(j, a) for a in planes}
+            q = [q_t[g, here, :] for g in range(4)]
+            rows = [weights[a] * (q[0] + float(a) * q[1] if a else q[0]) for a in planes]
+            rows += [weights[a] * q[2] for a in planes]
+            rows += [weights[a] * q[3] for a in planes]
+            high, low = halves(jnp.concatenate(rows, axis=0))
+            target[0:count, pl.ds(128 * j, 128)] = high
+            target[count : 2 * count, pl.ds(128 * j, 128)] = low
+
+        def sum_nodes(planes, source):
+            count, group = 24 * len(planes), 8 * len(planes)
+            totals = []
+            for b in range(LIVE):
+                summed = lax.dot_general(
+                    source[:, pl.ds(PPB * b, PPB)], w_s[b], (((1,), (1,)), ((), ())),
+                    preferred_element_type=F32,
+                )
+                totals.append(
+                    summed[0:count, 0:128] + summed[0:count, 128:256] + summed[count : 2 * count, 0:128]
+                )
+            for h in range(2):
+                both = jnp.where(left_half, totals[2 * h], totals[2 * h + 1])
+                both = both[0:group] + node_y * both[group : 2 * group] + node_z * both[2 * group :]
+                for i, a in enumerate(planes):
+                    part_s[step, pl.ds(8 * a, 8), pl.ds(128 * h, 128)] = both[8 * i : 8 * i + 8]
+
         for j in range(TILES):
             b, part = j // 4, pl.ds(128 * (j % 4), 128)
             here = pl.ds(8 * j, 8)
@@ -272,24 +303,9 @@
             w_s[b, 64:112, part] = high
             w_s[b, 128:176, part] = low
             w_s[b, 192:240, part] = low
-            weights = [wx_of(j, a) for a in range(6)]
-            q = [q_t[g, here, :] for g in range(4)]
-            rows = [weights[a] * (q[0] + float(a) * q[1] if a else q[0]) for a in range(6)]
-            rows += [weights[a] * q[2] for a in range(6)]
-            rows += [weights[a] * q[3] for a in range(6)]
-            high, low = halves(jnp.concatenate(rows, axis=0))
-            lh_s[0:144, pl.ds(128 * j, 128)] = high
-            lh_s[144:288, pl.ds(128 * j, 128)] = low
-
-        totals = []
-        for b in range(LIVE):
-            summed = lax.dot_general(
-                lh_s[:, pl.ds(PPB * b, PPB)], w_s[b], (((1,), (1,)), ((), ())), preferred_element_type=F32
-            )
-            totals.append(summed[0:144, 0:128] + summed[0:144, 128:256] + summed[144:288, 0:128])
-        for h in range(2):
-            both = jnp.where(left_half, totals[2 * h], totals[2 * h + 1])
-            part_s[step, :, pl.ds(128 * h, 128)] = both[0:48] + node_y * both[48:96] + node_z * both[96:144]
+            fill(j, SHARED_PLANES, lh_s)
+
+        sum_nodes(SHARED_PLANES, lh_s)
 
         sends = [
             pltpu.make_async_remote_copy(
@@ -303,6 +319,10 @@
         ]
         start_near(sends)
         near_sends.append(sends)
+
+        for j in range(TILES):
+            fill(j, INNER_PLANES, lh_inner)
+        sum_nodes(INNER_PLANES, lh_inner)
 
         def merged(value, which):
             high, low = halves(value)
@@ -326,6 +346,12 @@
             planes[k] = planes[k] + lower_planes[8 * k : 8 * k + 8]
             planes[4 + k] = planes[4 + k] + upper_planes[8 * k : 8 * k + 8]
 
+        still, driven = [], []
+        for a in range(6):
+            node_mass = jnp.maximum(planes[a][3:4], mass_floor)
+            still.append(planes[a] / node_mass)
+            driven.append(pltpu.roll(still[a], 4, 0) + gravity)
+
         pltpu.make_async_copy(got.at[step], got.at[step], top_recv.at[step]).wait()
         fastest = jnp.maximum(top[step], jnp.max(got[step], axis=0))
         fastest = jnp.max(fastest, axis=1, keepdims=True)
@@ -334,9 +360,7 @@
         node_rows, moments = [], []
         for a in range(6):
             here = pl.ds(8 * a, 8)
-            node_mass = jnp.maximum(planes[a][3:4], mass_floor)
-            momentum = planes[a] + dt * pltpu.roll(planes[a], 4, 0)
-            g = momentum / node_mass + dt * gravity
+            g = still[a] + dt * driven[a]
             g = jnp.minimum(jnp.maximum(g, low_s[here, :]), high_s[here, :])
             node_rows.append(g + pltpu.roll(g * node_y_wide, 4, 0))
             moments.append(g * node_z_wide)
@@ -445,7 +469,8 @@
             pltpu.VMEM((8 * TILES, 128), F32),
             pltpu.VMEM((4, 8 * TILES, 128), F32),
             pltpu.VMEM((LIVE, 256, PPB), BF16),
-            pltpu.VMEM((288, PARTICLES), BF16),
+            pltpu.VMEM((192, PARTICLES), BF16),
+            pltpu.VMEM((96, PARTICLES), BF16),
             pltpu.VMEM((STEPS, 48, 256), F32),
             pltpu.VMEM((3, 256, 512), BF16),
             pltpu.VMEM((48, 512), F32),

time: 31.4 us -> 31.1 us (level)
  no operation moved by 1% of the time
where the time goes in v4:
time: 31.1 us; the launch traced here: 31 us
  Pallas kernels  29.7 us (95%)
  between operations  1.29 us (4%)
    pallas_call x1, Pallas kernels, local(): pl.pallas_call(kernel, out_shape=[pltpu.VMEM((rows, PARTICLES), F32) for...  28.8 us
    pallas_call x1, Pallas kernels, local(): pl.pallas_call(spread_out, out_shape=[jax.ShapeDtypeStruct((rows, total),...  0.9 us

profile of v4, /device:TPU:1, one launch (start us, length us, event | category | flops | bytes accessed | tf_op | source)
XLA Modules:
  0.0 31.0 jit_solution(10567107429220887277)
XLA Ops:
  1.3 28.8 %material_points.1 = (f32[3,2048]{1,0:T(4,128)S(1)}, f32[3,2048]{1,0:T(4,128)S(1)}, f32[9,2048]{1,0:T(8,128)S(1)}, f32[9,2048]{1,0:T(8,128)S(1)}) custom-call(f32[3,4096]{1,0:T(4,128)} %pos.1, f32[3,4096]{1,0:T(4,128)} %vel.1, f32[9,4096]{1,0:T(8,128)} %dfm.1, f32[9,4096]{1,0:T(8,128)} %aff.1, f32[32,128]{1,0:T(8,128)} %bitcast.4, f32[32,128]{1,0:T(8,128)} %bitcast.5, ...), custom_call_target="tpu_custom_call" | custom-call | tf_op jit(solution)/shard_map/material_points/pallas_call | solution.py:450
  30.1 0.9 %spread_out.1 = (f32[3,4096]{1,0:T(4,128)}, f32[3,4096]{1,0:T(4,128)}, f32[9,4096]{1,0:T(8,128)}, f32[9,4096]{1,0:T(8,128)}) custom-call(f32[3,2048]{1,0:T(4,128)S(1)} %get-tuple-element.8.d, f32[3,2048]{1,0:T(4,128)S(1)} %get-tuple-element.9.v, f32[9,2048]{1,0:T(8,128)S(1)} %get-tuple-element.10.f, f32[9,2048]{1,0:T(8,128)S(1)} %get-tuple-element.11.c), custom_call_target="tpu_custom_call" | custom-call | tf_op jit(solution)/shard_map/spread_out/pallas_call | solution.py:499

commit v5 on v4

--- a/solution.py
+++ b/solution.py
@@ -130,11 +130,15 @@
     def find_top(step, v):
         squared = jnp.where(m > 0.0, v[0] * v[0] + v[1] * v[1] + v[2] * v[2], 0.0)
         top[step] = jnp.max(squared, axis=0, keepdims=True)
+        got[step, pl.ds(len(PEERS), 1), :] = top[step]
+
+    def arrived(step):
+        return got.at[step, pl.ds(0, len(PEERS)), :]
 
     def send_top(step):
         for k, peer in enumerate(peers):
             pltpu.make_async_remote_copy(
-                top.at[step], got.at[step, k], top_send.at[step], top_recv.at[step],
+                top.at[step], got.at[step, pl.ds(k, 1), :], top_send.at[step], top_recv.at[step],
                 device_id=(peer,), device_id_type=MESH,
             ).start()
 
@@ -352,8 +356,8 @@
             still.append(planes[a] / node_mass)
             driven.append(pltpu.roll(still[a], 4, 0) + gravity)
 
-        pltpu.make_async_copy(got.at[step], got.at[step], top_recv.at[step]).wait()
-        fastest = jnp.maximum(top[step], jnp.max(got[step], axis=0))
+        pltpu.make_async_copy(arrived(step), arrived(step), top_recv.at[step]).wait()
+        fastest = jnp.max(got[step], axis=0, keepdims=True)
         fastest = jnp.max(fastest, axis=1, keepdims=True)
         dt = courant / (jnp.sqrt(fastest) + sound_speed)
 
@@ -424,7 +428,7 @@
         pl.when(me < 127)(pair[0].wait_send)
         pl.when(me > 0)(pair[1].wait_send)
     for step in range(STEPS):
-        pltpu.make_async_copy(got.at[step], got.at[step], top_send.at[step]).wait()
+        pltpu.make_async_copy(arrived(step), arrived(step), top_send.at[step]).wait()
 
 
 def spread_out(d, v, f, c, o_d, o_v, o_f, o_c, nothing, sems):
@@ -478,7 +482,7 @@
             pltpu.VMEM((8, 128), jnp.int32),
             pltpu.VMEM((2, 8, 128), jnp.int32),
             pltpu.VMEM((STEPS, 1, 128), F32),
-            pltpu.VMEM((STEPS, len(PEERS), 1, 128), F32),
+            pltpu.VMEM((STEPS, len(PEERS) + 1, 128), F32),
             pltpu.VMEM((STEPS, 16, 256), F32),
             pltpu.VMEM((STEPS, 16, 256), F32),
             pltpu.SemaphoreType.DMA((8,)),

time: 31.1 us -> 31 us (level)
  no operation moved by 1% of the time
where the time goes in v5:
time: 31 us; the launch traced here: 30.9 us
  Pallas kernels  29.6 us (95%)
  between operations  1.29 us (4%)
    pallas_call x1, Pallas kernels, local(): pl.pallas_call(kernel, out_shape=[pltpu.VMEM((rows, PARTICLES), F32) for...  28.7 us
    pallas_call x1, Pallas kernels, local(): pl.pallas_call(spread_out, out_shape=[jax.ShapeDtypeStruct((rows, total),...  0.9 us

profile of v5, /device:TPU:1, one launch (start us, length us, event | category | flops | bytes accessed | tf_op | source)
XLA Modules:
  0.0 30.9 jit_solution(6609145205638193712)
XLA Ops:
  1.3 28.7 %material_points.1 = (f32[3,2048]{1,0:T(4,128)S(1)}, f32[3,2048]{1,0:T(4,128)S(1)}, f32[9,2048]{1,0:T(8,128)S(1)}, f32[9,2048]{1,0:T(8,128)S(1)}) custom-call(f32[3,4096]{1,0:T(4,128)} %pos.1, f32[3,4096]{1,0:T(4,128)} %vel.1, f32[9,4096]{1,0:T(8,128)} %dfm.1, f32[9,4096]{1,0:T(8,128)} %aff.1, f32[32,128]{1,0:T(8,128)} %bitcast.4, f32[32,128]{1,0:T(8,128)} %bitcast.5, ...), custom_call_target="tpu_custom_call" | custom-call | tf_op jit(solution)/shard_map/material_points/pallas_call | solution.py:454
  30.0 0.9 %spread_out.1 = (f32[3,4096]{1,0:T(4,128)}, f32[3,4096]{1,0:T(4,128)}, f32[9,4096]{1,0:T(8,128)}, f32[9,4096]{1,0:T(8,128)}) custom-call(f32[3,2048]{1,0:T(4,128)S(1)} %get-tuple-element.8.d, f32[3,2048]{1,0:T(4,128)S(1)} %get-tuple-element.9.v, f32[9,2048]{1,0:T(8,128)S(1)} %get-tuple-element.10.f, f32[9,2048]{1,0:T(8,128)S(1)} %get-tuple-element.11.c), custom_call_target="tpu_custom_call" | custom-call | tf_op jit(solution)/shard_map/spread_out/pallas_call | solution.py:503
